TPU v7x, 32 devices: a whole 2x2x4 slice. The times are simulated.
32 devices in a mesh: freq: 4 (over y, x), space: 8 (over z, core).
Axes of the slice: x: 2, y: 2, z: 4, core: 2. Of those that a mesh axis runs over, the one named last changes fastest.
Arguments:
- spectra: bfloat16 [64, 24576, 256], P('freq', 'space'), may hold values from -48 to 48, as said below
- weight: float32 [24576], P('space'), may hold values from 0.25 to 4
- partner: int32 [64], P('freq'), may hold values from 0 to 15
- counts: int32 [64], P('freq'), may hold values from 1 to 8
Outputs:
- modes: bfloat16 [64, 16, 24576], P('freq', None, 'space')
- energy: float32 [64, 8], P('freq')
- coherence: float32 [64, 2, 8, 8], P('freq')
Inputs may be any that keep to these rules, and one draw needn't show every extreme that they name: spectra are finite Fourier coefficients.
All inputs are finite; a program needn't handle non-finite values.
Results may differ from a plain program's by a relative error of at most 0.0045.
Values may be sent and summed in bfloat16 or wider, within the bound.
A program may use at most 128 MiB of HBM per device.

v0:
```python
import jax
import jax.numpy as jnp
from jax import lax
from jax.sharding import PartitionSpec as P

KMAX = 8
ITERS = 4


def from_partner(block, axis, apart):
    count = lax.axis_size(axis)
    route = []
    for low in range(count):
        high = low | 1 << apart
        if high != low and high < count:
            route += [(low, high), (high, low)]
    return lax.ppermute(block, axis, route)


def embed(gram_re, gram_im):
    top = jnp.concatenate([gram_re, -gram_im], axis=2)
    bottom = jnp.concatenate([gram_im, gram_re], axis=2)
    return jnp.concatenate([top, bottom], axis=1)


def apply_operator(operator, basis):
    return jnp.einsum("fkc,fdc->fkd", basis, operator, precision=lax.Precision.HIGHEST)


def orthonormal(vectors, half):
    done = []
    for index in range(vectors.shape[1]):
        vector = vectors[:, index, :]
        for earlier in done:
            early_re, early_im = (earlier[:, :half], earlier[:, half:])
            vec_re, vec_im = (vector[:, :half], vector[:, half:])
            proj_re = jnp.sum(early_re * vec_re + early_im * vec_im, axis=1, keepdims=True)
            proj_im = jnp.sum(early_re * vec_im - early_im * vec_re, axis=1, keepdims=True)
            new_re = vec_re - proj_re * early_re + proj_im * early_im
            new_im = vec_im - proj_re * early_im - proj_im * early_re
            vector = jnp.concatenate([new_re, new_im], axis=1)
        length = jnp.sqrt(jnp.sum(vector * vector, axis=1, keepdims=True) + 1e-06)
        done.append(vector / length)
    return jnp.stack(done, axis=1)


def solve(gram_re, gram_im):
    half = gram_re.shape[1]
    operator = embed(gram_re, gram_im)
    basis = jnp.broadcast_to(
        jnp.eye(KMAX, 2 * half, dtype=jnp.float32), (gram_re.shape[0], KMAX, 2 * half)
    )
    for sweep in range(ITERS):
        basis = orthonormal(apply_operator(operator, basis), half)
    image = apply_operator(operator, basis)
    energy = jnp.sum(basis * image, axis=2)
    return (basis, energy)


def combine(moments, half, total):
    gram_re = (moments[:, :half, :half] + moments[:, half:, half:]) / total
    gram_im = (moments[:, :half, half:] - moments[:, half:, :half]) / total
    return (gram_re, gram_im)


def coefficients(basis, energy, counts):
    half = basis.shape[2] // 2
    ranks = jnp.arange(KMAX, dtype=jnp.int32)[None, :]
    scale = jnp.where(ranks < counts[:, None], 1.0 / jnp.sqrt(energy + 1e-06), 0.0)[:, :, None]
    part_re, part_im = (basis[:, :, :half], basis[:, :, half:])
    upper = jnp.concatenate([part_re, -part_im], axis=2) * scale
    lower = jnp.concatenate([part_im, part_re], axis=2) * scale
    return jnp.concatenate([upper, lower], axis=1).astype(jnp.bfloat16)


def cross_terms(own_modes, other_modes, point_weight, total):
    phi = own_modes.astype(jnp.float32)
    psi = other_modes.astype(jnp.float32)
    wphi = phi * point_weight[None, None, :]
    highest = lax.Precision.HIGHEST

    def inner(left, right):
        return jnp.einsum("fkp,flp->fkl", left, right, precision=highest)

    real_part = inner(wphi[:, :KMAX], psi[:, :KMAX]) + inner(wphi[:, KMAX:], psi[:, KMAX:])
    imag_part = inner(wphi[:, :KMAX], psi[:, KMAX:]) - inner(wphi[:, KMAX:], psi[:, :KMAX])
    return jnp.stack([real_part, imag_part], axis=1) / total


def on_device(spectra, weight, partner, counts):
    groups = spectra.shape[0]
    half = spectra.shape[2] // 2
    total = spectra.shape[1] * lax.axis_size("space")
    weighted = (weight[None, :, None] * spectra).astype(jnp.bfloat16)
    moments = lax.dot_general(
        spectra, weighted, (((1,), (1,)), ((0,), (0,))), preferred_element_type=jnp.float32
    )
    summed = lax.psum(moments, "space")
    gram_re, gram_im = combine(summed, half, total)
    basis, energy = solve(gram_re, gram_im)
    coefficient = coefficients(basis, energy, counts)
    modes = jnp.einsum(
        "fkc,fpc->fkp", coefficient, spectra, preferred_element_type=jnp.float32
    ).astype(jnp.bfloat16)
    levels = lax.axis_size("freq").bit_length() - 1
    mirrored = modes
    for bit in range(levels):
        mirrored = from_partner(mirrored, "freq", bit)
    match = (partner[:, None] == jnp.arange(groups, dtype=jnp.int32)[None, :]).astype(jnp.bfloat16)
    chosen = jnp.einsum("fg,gkp->fkp", match, mirrored, preferred_element_type=jnp.float32).astype(
        jnp.bfloat16
    )
    local = cross_terms(modes, chosen, weight, total)
    coherence = lax.psum(local, "space")
    return (modes, energy, coherence)


def solution(mesh):
    in_specs = (P("freq", "space", None), P("space"), P("freq"), P("freq"))
    out_specs = (P("freq", None, "space"), P("freq", None), P("freq", None, None, None))
    return jax.shard_map(
        on_device, mesh=mesh, in_specs=in_specs, out_specs=out_specs, check_vma=False
    )
```

profile of v0, /device:TPU:0, one launch (start us, length us, event | category | flops | bytes accessed | tf_op | source)
XLA Modules:
  0.0 290.2 jit_solution(2149110146235932898)
XLA Ops:
  7.2 20.7 %fusion.2 = f32[16,256,256]{1,2,0:T(8,128)} fusion(bf16[16,3072,256]{2,1,0:T(8,128)(2,1)} %param.4, f32[3072]{0:T(1024)} %param.5), kind=kOutput, calls=%fused_computation.7 | convolution fusion | flops 6480199680 | bytes 29372416 | tf_op jit(solution)/shard_map/dot_general | solution.py:95
  27.9 99.3 %all-reduce.2.cloned.1.call-done = f32[16,256,256]{1,2,0:T(8,128)} async-done(((f32[16,256,256]{1,2,0:T(8,128)}), f32[16,256,256]{1,2,0:T(8,128)}) %all-reduce.2.cloned.1.call-update) | async-done | bytes 4194320 | tf_op jit(solution)/shard_map/psum | solution.py:98
  127.2 2.8 fusion.80
  130.0 1.9 fusion.42
  132.7 0.3 add_reduce_fusion.96
  133.0 0.3 add_reduce_fusion.95
  133.6 0.3 add_reduce_fusion.89
  134.4 0.3 add_reduce_fusion.88
  135.1 0.3 add_reduce_fusion.87
  135.4 0.3 add_reduce_fusion.86
  136.0 0.2 add_reduce_fusion.85
  137.4 2.0 fusion.40
  140.2 0.3 add_reduce_fusion.68
  140.5 0.3 add_reduce_fusion.67
  141.1 0.3 add_reduce_fusion.61
  141.9 0.3 add_reduce_fusion.60
  142.7 0.3 add_reduce_fusion.59
  142.9 0.3 add_reduce_fusion.58
  143.5 0.2 add_reduce_fusion.57
  145.0 2.0 fusion.38
  147.8 0.3 add_reduce_fusion.40
  148.1 0.3 add_reduce_fusion.39
  148.6 0.3 add_reduce_fusion.33
  149.4 0.3 add_reduce_fusion.32
  150.2 0.3 add_reduce_fusion.31
  150.5 0.3 add_reduce_fusion.30
  151.0 0.2 add_reduce_fusion.29
  152.5 2.2 fusion.36
  155.5 0.3 add_reduce_fusion.12
  155.8 0.3 add_reduce_fusion.11
  156.4 0.3 add_reduce_fusion.5
  157.2 0.3 add_reduce_fusion.4
  157.9 0.3 add_reduce_fusion.3
  158.2 0.3 add_reduce_fusion.2
  158.8 0.2 add_reduce_fusion.1
  160.3 2.0 fusion.34
  162.5 12.4 %convert_multiply_fusion = (f32[16,16,3072]{2,1,0:T(8,128)S(1)}, bf16[16,16,3072]{2,1,0:T(8,128)(2,1)}) fusion(f32[3072]{0:T(1024)S(1)} %copy-done, bf16[16,3072,256]{2,1,0:T(8,128)(2,1)} %param.4, bf16[16,16,256]{2,0,1:T(8,128)(2,1)S(1)} %pad_maximum_fusion), kind=kOutput, calls=%fused_computation.6 | convolution fusion | flops 405012480 | bytes 30027776 | tf_op jit(solution)/shard_map/fkc,fpc->fkp/dot_general | solution.py:102
  175.0 1.5 collective-permute-start
  176.5 34.6 %collective-permute-done = bf16[16,16,3072]{2,1,0:T(8,128)(2,1)S(1)} collective-permute-done((bf16[16,16,3072]{2,1,0:T(8,128)(2,1)}, bf16[16,16,3072]{2,1,0:T(8,128)(2,1)S(1)}, u32[]{:S(2)}, u32[]{:S(2)}) %collective-permute-start) | collective-permute-done | bytes 1572896 | tf_op jit(solution)/shard_map/ppermute | solution.py:17
  211.1 1.5 collective-permute-start.1
  212.6 33.6 %collective-permute-done.1 = bf16[16,16,3072]{2,1,0:T(8,128)(2,1)S(1)} collective-permute-done((bf16[16,16,3072]{2,1,0:T(8,128)(2,1)S(1)}, bf16[16,16,3072]{2,1,0:T(8,128)(2,1)S(1)}, u32[]{:S(2)}, u32[]{:S(2)}) %collective-permute-start.1) | collective-permute-done | bytes 1572896 | tf_op jit(solution)/shard_map/ppermute | solution.py:17
  246.1 1.9 convolution_convert_fusion
  248.1 1.8 fusion.6
  249.9 1.8 fusion.4
  251.7 1.5 fusion.15
  253.2 1.8 fusion.21
  255.0 27.5 %psum.15 = f32[16,2,8,8]{3,2,0,1:T(8,128)S(1)} all-reduce(f32[16,2,8,8]{3,2,0,1:T(8,128)S(1)} %maximum_multiply_fusion.2), channel_id=1, replica_groups=mesh['freq'=4,'space'=8] {'space'}, use_global_device_ids=true, to_apply=%region_258.259 | all-reduce | flops 2048 | bytes 16384 | tf_op jit(solution)/shard_map/psum | solution.py:114
  282.6 0.7 copy.52
  (215 shorter events, 14.6 us)
Async XLA Ops:
  7.2 120.1 %all-reduce.2.cloned.1.call-start = ((), (), s32[]{:S(2)}) async-start(), calls=%async_computation | async-start | bytes 8388608 | tf_op jit(solution)/shard_map/psum | solution.py:98
  158.5 3.9 %copy-start.2 = (s32[16]{0:T(128)S(1)}, s32[16]{0:T(128)}, u32[]{:S(2)}) copy-start(s32[16]{0:T(128)} %param.7) | copy-start | bytes 196
  160.0 2.6 copy-start
  162.4 12.6 %copy-start.1 = (f32[16,8]{0,1:T(8,128)}, f32[16,8]{0,1:T(8,128)S(1)}, u32[]{:S(2)}) copy-start(f32[16,8]{0,1:T(8,128)S(1)} %fusion.33) | copy-start | bytes 1540
  162.5 83.6 %copy-start.3 = (s32[16]{0:T(128)S(1)}, s32[16]{0:T(128)}, u32[]{:S(2)}) copy-start(s32[16]{0:T(128)} %param.6) | copy-start | bytes 196
  175.0 36.1 %collective-permute-start = (bf16[16,16,3072]{2,1,0:T(8,128)(2,1)}, bf16[16,16,3072]{2,1,0:T(8,128)(2,1)S(1)}, u32[]{:S(2)}, u32[]{:S(2)}) collective-permute-start(bf16[16,16,3072]{2,1,0:T(8,128)(2,1)} %get-tuple-element.649), channel_id=1, source_target_pairs={{0,8},{8,0},{16,24},{24,16},{1,9},{9,1},{17,25},{25,17},{2,10},{10... | collective-permute-start | bytes 4718600 | tf_op jit(solution)/shard_map/ppermute | solution.py:17
  211.1 35.0 %collective-permute-start.1 = (bf16[16,16,3072]{2,1,0:T(8,128)(2,1)S(1)}, bf16[16,16,3072]{2,1,0:T(8,128)(2,1)S(1)}, u32[]{:S(2)}, u32[]{:S(2)}) collective-permute-start(bf16[16,16,3072]{2,1,0:T(8,128)(2,1)S(1)} %collective-permute-done), channel_id=1, source_target_pairs={{0,16},{16,0},{8,24},{24,8},{1,17},{17,1},{9,25},{25,9},{2,18},{18... | collective-permute-start | bytes 4718600 | tf_op jit(solution)/shard_map/ppermute | solution.py:17
Sparse Core Ops, SparseCore 0:
  28.0 99.1 all-reduce.1
where the time goes:
time: 290 us
  waiting for transfers between devices  168 us (58%)
  matrix products  51.8 us (18%)
  blocking collectives  27.5 us (9%)
  other arithmetic  24.4 us (8%)
  between operations  14.6 us (5%)
  starting transfers between devices  2.98 us (1%)
    psum x1, waiting for transfers between devices, on_device(): summed = lax.psum(moments, 'space')  99.3 us
    ppermute x2, waiting for transfers between devices, from_partner(): return lax.ppermute(block, axis, route)  68.2 us
    psum x1, blocking collectives, on_device(): coherence = lax.psum(local, 'space')  27.5 us
    dot_general x1, matrix products, on_device(): lax.dot_general(spectra, weighted, (((1,), (1,)), ((0,), (0,))), preferre...  20.7 us
    dot_general x1, matrix products, on_device(): jnp.einsum('fkc,fpc->fkp', coefficient, spectra, preferred_element_type=j...  12.4 us
    reduce_sum x44, other arithmetic, orthonormal(): jnp.sum(early_re * vec_re + early_im * vec_im, axis=1, keepdims=True)  10.6 us
    dot_general x5, matrix products, apply_operator(): jnp.einsum('fkc,fdc->fkd', basis, operator, precision=lax.Precision.HIGHEST)  9.94 us
    dot_general x4, matrix products, inner(): return jnp.einsum('fkp,flp->fkl', left, right, precision=highest)  6.86 us
  transfers between devices with their start and end apart: 3, of which 3 were waited for; matrix products, arithmetic and copies ran while one was open for 0% of the time, Pallas kernels for 0%

commit v1 on v0

--- a/solution.py
+++ b/solution.py
@@ -95,7 +95,7 @@
     moments = lax.dot_general(
         spectra, weighted, (((1,), (1,)), ((0,), (0,))), preferred_element_type=jnp.float32
     )
-    summed = lax.psum(moments, "space")
+    summed = jnp.sum(lax.all_gather(moments, "space"), axis=0)
     gram_re, gram_im = combine(summed, half, total)
     basis, energy = solve(gram_re, gram_im)
     coefficient = coefficients(basis, energy, counts)

time: 290 us -> 511 us (1.76)
  waiting for transfers between devices: 168 us -> 361 us
  other arithmetic: 24.4 us -> 38.9 us
  matrix products: 51.8 us -> 59.5 us
  local copies, waits for them, and re-layouts: 1.36 us -> 6.78 us
    all_gather x0 -> x1, waiting for transfers between devices: none -> 291 us  [on_device(): summed = jnp.sum(lax.all_gather(moments, 'space'), axis=0)]
    psum x1 -> x0, waiting for transfers between devices: 99.3 us -> none  [on_device(): summed = lax.psum(moments, 'space')]
    reduce_sum x0 -> x1, other arithmetic: none -> 14.5 us  [on_device(): summed = jnp.sum(lax.all_gather(moments, 'space'), axis=0)]
    dot_general x5, matrix products: 9.94 us -> 17.8 us  [apply_operator(): jnp.einsum('fkc,fdc->fkd', basis, operator, precision=lax.Precision.HIGHEST)]
    dot_general x0 -> x1, local copies, waits for them, and re-layouts: none -> 5.39 us  [on_device(): lax.dot_general(spectra, weighted, (((1,), (1,)), ((0,), (0,))), preferre...]
where the time goes in v1:
time: 511 us
  waiting for transfers between devices  361 us (71%)
  matrix products  59.5 us (12%)
  other arithmetic  38.9 us (8%)
  blocking collectives  27.3 us (5%)
  between operations  14.6 us (3%)
  local copies, waits for them, and re-layouts  6.78 us (1%)
    all_gather x1, waiting for transfers between devices, on_device(): summed = jnp.sum(lax.all_gather(moments, 'space'), axis=0)  291 us
    ppermute x2, waiting for transfers between devices, from_partner(): return lax.ppermute(block, axis, route)  69.5 us
    psum x1, blocking collectives, on_device(): coherence = lax.psum(local, 'space')  27.3 us
    dot_general x1, matrix products, on_device(): lax.dot_general(spectra, weighted, (((1,), (1,)), ((0,), (0,))), preferre...  20.6 us
    dot_general x5, matrix products, apply_operator(): jnp.einsum('fkc,fdc->fkd', basis, operator, precision=lax.Precision.HIGHEST)  17.8 us
    reduce_sum x1, other arithmetic, on_device(): summed = jnp.sum(lax.all_gather(moments, 'space'), axis=0)  14.5 us
    dot_general x1, matrix products, on_device(): jnp.einsum('fkc,fpc->fkp', coefficient, spectra, preferred_element_type=j...  12.4 us
    reduce_sum x44, other arithmetic, orthonormal(): jnp.sum(early_re * vec_re + early_im * vec_im, axis=1, keepdims=True)  10.6 us
  transfers between devices with their start and end apart: 3, of which 3 were waited for; matrix products, arithmetic and copies ran while one was open for 0% of the time, Pallas kernels for 0%

profile of v1, /device:TPU:0, one launch (start us, length us, event | category | flops | bytes accessed | tf_op | source)
XLA Modules:
  0.0 511.1 jit_solution(1717100442794676299)
XLA Ops:
  7.2 20.6 %fusion.2 = f32[16,256,256]{1,2,0:T(8,128)} fusion(bf16[16,3072,256]{2,1,0:T(8,128)(2,1)} %param.4, f32[3072]{0:T(1024)} %param.5), kind=kOutput, calls=%fused_computation.7 | convolution fusion | flops 6480199680 | bytes 29372416 | tf_op jit(solution)/shard_map/dot_general | solution.py:95
  27.8 5.4 %copy.49 = f32[16,256,256]{2,1,0:T(8,128)} copy(f32[16,256,256]{1,2,0:T(8,128)} %fusion.2) | data formatting | bytes 8388608 | tf_op jit(solution)/shard_map/dot_general | solution.py:95
  33.3 291.5 %all-gather.3.cloned.1.call-done = f32[128,256,256]{2,1,0:T(8,128)} async-done(((f32[16,256,256]{2,1,0:T(8,128)}), f32[128,256,256]{2,1,0:T(8,128)}) %all-gather.3.cloned.1.call-update) | async-done | bytes 33554448 | tf_op jit(solution)/shard_map/all_gather | solution.py:98
  324.7 14.5 %reduce_sum.2322 = f32[16,256,256]{2,1,0:T(8,128)} reduce(f32[8,16,256,256]{3,2,1,0:T(8,128)} %bitcast.166, f32[]{:T(128)} %constant.3.clone.1), dimensions={0}, to_apply=%region_0.0 | reduce | flops 7340032 | bytes 37748740 | tf_op jit(solution)/shard_map/reduce_sum | solution.py:98
  339.3 2.8 fusion.80
  342.0 3.4 fusion.42
  346.3 0.3 add_reduce_fusion.96
  346.6 0.3 add_reduce_fusion.95
  347.2 0.3 add_reduce_fusion.89
  348.0 0.3 add_reduce_fusion.88
  348.7 0.3 add_reduce_fusion.87
  349.0 0.3 add_reduce_fusion.86
  349.6 0.2 add_reduce_fusion.85
  351.0 3.5 fusion.40
  355.4 0.3 add_reduce_fusion.68
  355.7 0.3 add_reduce_fusion.67
  356.3 0.3 add_reduce_fusion.61
  357.1 0.3 add_reduce_fusion.60
  357.8 0.3 add_reduce_fusion.59
  358.1 0.3 add_reduce_fusion.58
  358.7 0.2 add_reduce_fusion.57
  360.1 3.7 fusion.38
  364.7 0.3 add_reduce_fusion.40
  365.0 0.3 add_reduce_fusion.39
  365.6 0.3 add_reduce_fusion.33
  366.4 0.3 add_reduce_fusion.32
  367.1 0.3 add_reduce_fusion.31
  367.4 0.3 add_reduce_fusion.30
  369.4 3.5 fusion.36
  373.8 0.3 add_reduce_fusion.12
  374.1 0.3 add_reduce_fusion.11
  374.7 0.3 add_reduce_fusion.5
  375.5 0.3 add_reduce_fusion.4
  376.2 0.3 add_reduce_fusion.3
  376.5 0.3 add_reduce_fusion.2
  378.6 3.5 fusion.34
  382.4 12.4 %convert_multiply_fusion = (f32[16,16,3072]{2,1,0:T(8,128)S(1)}, bf16[16,16,3072]{2,1,0:T(8,128)(2,1)}) fusion(f32[3072]{0:T(1024)S(1)} %copy-done, bf16[16,3072,256]{2,1,0:T(8,128)(2,1)} %param.4, bf16[16,16,256]{2,0,1:T(8,128)(2,1)S(1)} %pad_maximum_fusion), kind=kOutput, calls=%fused_computation.6 | convolution fusion | flops 405012480 | bytes 30027776 | tf_op jit(solution)/shard_map/fkc,fpc->fkp/dot_general | solution.py:102
  394.9 1.5 collective-permute-start
  396.3 35.3 %collective-permute-done = bf16[16,16,3072]{2,1,0:T(8,128)(2,1)S(1)} collective-permute-done((bf16[16,16,3072]{2,1,0:T(8,128)(2,1)}, bf16[16,16,3072]{2,1,0:T(8,128)(2,1)S(1)}, u32[]{:S(2)}, u32[]{:S(2)}) %collective-permute-start) | collective-permute-done | bytes 1572896 | tf_op jit(solution)/shard_map/ppermute | solution.py:17
  431.6 1.5 collective-permute-start.1
  433.1 34.2 %collective-permute-done.1 = bf16[16,16,3072]{2,1,0:T(8,128)(2,1)S(1)} collective-permute-done((bf16[16,16,3072]{2,1,0:T(8,128)(2,1)S(1)}, bf16[16,16,3072]{2,1,0:T(8,128)(2,1)S(1)}, u32[]{:S(2)}, u32[]{:S(2)}) %collective-permute-start.1) | collective-permute-done | bytes 1572896 | tf_op jit(solution)/shard_map/ppermute | solution.py:17
  467.3 1.9 convolution_convert_fusion
  469.3 1.8 fusion.6
  471.1 1.8 fusion.4
  472.9 1.5 fusion.15
  474.4 1.8 fusion.21
  476.2 27.3 %psum.7 = f32[16,2,8,8]{3,2,0,1:T(8,128)S(1)} all-reduce(f32[16,2,8,8]{3,2,0,1:T(8,128)S(1)} %maximum_multiply_fusion.2), channel_id=1, replica_groups=mesh['freq'=4,'space'=8] {'space'}, use_global_device_ids=true, to_apply=%region_258.259 | all-reduce | flops 2048 | bytes 16384 | tf_op jit(solution)/shard_map/psum | solution.py:114
  503.5 0.7 copy.94
  (217 shorter events, 15.2 us)
Async XLA Ops:
  7.2 317.6 %all-gather.3.cloned.1.call-start = ((), (), s32[]{:S(2)}) async-start(), calls=%async_computation | async-start | bytes 37748736 | tf_op jit(solution)/shard_map/all_gather | solution.py:98
  376.8 5.4 %copy-start.2 = (s32[16]{0:T(128)S(1)}, s32[16]{0:T(128)}, u32[]{:S(2)}) copy-start(s32[16]{0:T(128)} %param.7) | copy-start | bytes 196
  378.3 4.1 copy-start
  382.2 12.6 %copy-start.1 = (f32[16,8]{0,1:T(8,128)}, f32[16,8]{0,1:T(8,128)S(1)}, u32[]{:S(2)}) copy-start(f32[16,8]{0,1:T(8,128)S(1)} %fusion.33) | copy-start | bytes 1540
  382.4 84.9 %copy-start.3 = (s32[16]{0:T(128)S(1)}, s32[16]{0:T(128)}, u32[]{:S(2)}) copy-start(s32[16]{0:T(128)} %param.6) | copy-start | bytes 196
  394.9 36.8 %collective-permute-start = (bf16[16,16,3072]{2,1,0:T(8,128)(2,1)}, bf16[16,16,3072]{2,1,0:T(8,128)(2,1)S(1)}, u32[]{:S(2)}, u32[]{:S(2)}) collective-permute-start(bf16[16,16,3072]{2,1,0:T(8,128)(2,1)} %get-tuple-element.652), channel_id=1, source_target_pairs={{0,8},{8,0},{16,24},{24,16},{1,9},{9,1},{17,25},{25,17},{2,10},{10... | collective-permute-start | bytes 4718600 | tf_op jit(solution)/shard_map/ppermute | solution.py:17
  431.6 35.7 %collective-permute-start.1 = (bf16[16,16,3072]{2,1,0:T(8,128)(2,1)S(1)}, bf16[16,16,3072]{2,1,0:T(8,128)(2,1)S(1)}, u32[]{:S(2)}, u32[]{:S(2)}) collective-permute-start(bf16[16,16,3072]{2,1,0:T(8,128)(2,1)S(1)} %collective-permute-done), channel_id=1, source_target_pairs={{0,16},{16,0},{8,24},{24,8},{1,17},{17,1},{9,25},{25,9},{2,18},{18... | collective-permute-start | bytes 4718600 | tf_op jit(solution)/shard_map/ppermute | solution.py:17
Sparse Core Ops, SparseCore 0:
  33.4 291.3 all-gather.2
